TPU v7x, 32 devices: a whole 2x2x4 slice. The times are simulated.
32 devices in a mesh: site: 2 (over x), row: 4 (over z), col: 4 (over y, core).
Axes of the slice: x: 2, y: 2, z: 4, core: 2. Of those that a mesh axis runs over, the one named last changes fastest.
Arguments:
- pair_array: bfloat16 [128, 64, 128], P(('site', 'row'), 'col'), parts along dimension 0, may hold values from -6 to 6
- in_gain: float32 [128], replicated, may hold values from 0.25 to 1.75
- left_weight: bfloat16 [256, 128], P('site'), parts along dimension 0, may hold values from -0.5 to 0.5
- right_weight: bfloat16 [256, 128], P('site'), parts along dimension 0, may hold values from -0.5 to 0.5
- mid_gain: float32 [128], replicated, may hold values from 0.25 to 1.75
- out_weight: bfloat16 [256, 128], P('site'), parts along dimension 0, may hold values from -0.5 to 0.5
- out_gate: bfloat16 [256, 128], P('site'), parts along dimension 0, may hold values from -0.5 to 0.5
Outputs:
- triangle_out: bfloat16 [128, 64, 128], P(('site', 'row'), 'col'), parts along dimension 0
There are 2 independent parts, one for each index of `site`. A program takes and returns all parts, laid end to end along the dimension named above; an argument that names none is the same for every part. Nothing has to cross between parts.
All inputs are finite; a program needn't handle non-finite values.
Results may differ from a plain program's by a relative error of at most 0.012.
Values may be sent and summed in bfloat16 or wider, within the bound.
A program may use at most 64 MiB of HBM per device.

v0:
```python
import jax
import jax.numpy as jnp
from jax import lax
from jax.sharding import PartitionSpec as P


def norm_channels(values, channel_gain):
    centred = values - jnp.mean(values, axis=-1, keepdims=True)
    return (
        centred
        * lax.rsqrt(jnp.mean(centred * centred, axis=-1, keepdims=True) + 1e-05)
        * channel_gain
    )


def both_factors(pair_in, in_gain, left_weight, right_weight):
    ready = norm_channels(pair_in.astype(jnp.float32), in_gain).astype(jnp.bfloat16)
    ready = lax.optimization_barrier(ready)
    left = jnp.einsum("ijc,cd->ijd", ready, left_weight, preferred_element_type=jnp.float32)
    right = jnp.einsum("ijc,cd->ijd", ready, right_weight, preferred_element_type=jnp.float32)
    return (ready, left.astype(jnp.bfloat16), right.astype(jnp.bfloat16))


def finish_pair(mixed, ready, mid_gain, out_weight, out_gate):
    scaled = norm_channels(mixed.astype(jnp.float32), mid_gain).astype(jnp.bfloat16)
    scaled = lax.optimization_barrier(scaled)
    gate = jax.nn.sigmoid(
        jnp.einsum("ijc,cd->ijd", ready, out_gate, preferred_element_type=jnp.float32)
    )
    return (
        jnp.einsum("ijd,dc->ijc", scaled, out_weight, preferred_element_type=jnp.float32) * gate
    ).astype(jnp.bfloat16)


def body(pair_array, in_gain, left_weight, right_weight, mid_gain, out_weight, out_gate):
    ready, left, right = both_factors(pair_array, in_gain, left_weight, right_weight)
    count = pair_array.shape[0] * lax.axis_size("row")
    left_lines, right_lines = (
        lax.all_to_all(left, "row", split_axis=2, concat_axis=0, tiled=True),
        lax.all_to_all(right, "row", split_axis=2, concat_axis=0, tiled=True),
    )
    strip = jnp.einsum(
        "kid,kjd->ijd",
        lax.all_gather(left_lines, "col", axis=1, tiled=True),
        right_lines,
        preferred_element_type=jnp.float32,
    )
    strip = (strip * count ** (-0.5)).astype(jnp.bfloat16)
    mixed = lax.all_to_all(strip, "row", split_axis=0, concat_axis=2, tiled=True)
    return finish_pair(mixed, ready, mid_gain, out_weight, out_gate)


def solution(mesh):
    return jax.shard_map(
        body,
        mesh=mesh,
        in_specs=(
            P(("site", "row"), "col", None),
            P(),
            P("site", None),
            P("site", None),
            P(),
            P("site", None),
            P("site", None),
        ),
        out_specs=P(("site", "row"), "col", None),
        check_vma=False,
    )
```

profile of v0, /device:TPU:0, one launch (start us, length us, event | category | flops | bytes accessed | tf_op | source)
XLA Modules:
  0.0 46.4 jit_solution(6474242782185736790)
XLA Ops:
  0.0 0.0 copy-start
  0.0 0.0 copy-start.1
  0.0 1.0 %convert_reduce_fusion = f32[16,16]{1,0:T(8,128)S(1)} fusion(bf16[16,16,128]{2,1,0:T(8,128)(2,1)} %param.7), kind=kLoop, calls=%fused_computation.15 | loop fusion | flops 65280 | bytes 66560 | tf_op jit(solution)/shard_map/reduce_sum | solution.py:8
  1.0 0.0 copy-done.1
  1.0 0.2 fusion.10
  1.2 0.0 copy-start.4
  1.3 0.6 %copy-done.4 = f32[128]{0:T(128)S(1)} copy-done((f32[128]{0:T(128)S(1)}, f32[128]{0:T(128)}, u32[]{:S(2)}) %copy-start.4) | copy-done | bytes 536
  1.9 0.1 fusion.12
  2.0 0.0 copy-done
  2.0 0.1 convolution_convert_fusion.1
  2.2 0.4 copy.32
  2.6 1.2 %reshape.39 = bf16[4,2,4096]{2,1,0:T(2,128)(2,1)} reshape(bf16[128,16,16]{2,1,0:T(8,128)(2,1)S(1)} %bitcast.43) | data formatting | bytes 131072
  3.8 0.0 copy-start.2
  3.8 6.5 %all-to-all-start = ((bf16[4,2,4096]{2,1,0:T(2,128)(2,1)}), bf16[4,2,4096]{2,1,0:T(2,128)(2,1)S(1)}, u32[]{:S(2)}, u32[]{:S(2)}) async-start(bf16[4,2,4096]{2,1,0:T(2,128)(2,1)} %reshape.39), calls=%async_computation | async-start | bytes 131072 | tf_op jit(solution)/shard_map/all_to_all | solution.py:40
  10.3 0.0 copy-done.2
  10.3 0.1 convolution_convert_fusion
  10.4 0.4 copy.34
  10.9 1.2 %reshape.41 = bf16[4,2,4096]{2,1,0:T(2,128)(2,1)} reshape(bf16[128,16,16]{2,1,0:T(8,128)(2,1)S(1)} %bitcast.44) | data formatting | bytes 131072
  12.0 4.0 %all-to-all-done = bf16[4,2,4096]{2,1,0:T(2,128)(2,1)S(1)} async-done(((bf16[4,2,4096]{2,1,0:T(2,128)(2,1)}), bf16[4,2,4096]{2,1,0:T(2,128)(2,1)S(1)}, u32[]{:S(2)}, u32[]{:S(2)}) %all-to-all-start) | async-done | bytes 65568 | tf_op jit(solution)/shard_map/all_to_all | solution.py:40
  16.0 3.3 %all-to-all-start.1 = ((bf16[4,2,4096]{2,1,0:T(2,128)(2,1)}), bf16[4,2,4096]{2,1,0:T(2,128)(2,1)S(1)}, u32[]{:S(2)}, u32[]{:S(2)}) async-start(bf16[4,2,4096]{2,1,0:T(2,128)(2,1)} %reshape.41), calls=%async_computation.1 | async-start | bytes 131072 | tf_op jit(solution)/shard_map/all_to_all | solution.py:39
  19.3 0.4 reshape.40
  19.7 0.4 copy.33
  20.2 0.3 copy.37
  20.5 4.6 %all-to-all-done.1 = bf16[4,2,4096]{2,1,0:T(2,128)(2,1)S(1)} async-done(((bf16[4,2,4096]{2,1,0:T(2,128)(2,1)}), bf16[4,2,4096]{2,1,0:T(2,128)(2,1)S(1)}, u32[]{:S(2)}, u32[]{:S(2)}) %all-to-all-start.1) | async-done | bytes 65568 | tf_op jit(solution)/shard_map/all_to_all | solution.py:39
  25.0 0.4 reshape.42
  25.4 0.4 copy.35
  25.9 0.3 copy.36
  26.2 7.2 %all_gather.3 = bf16[64,64,32]{0,1,2:T(8,128)(2,1)S(1)} all-gather(bf16[64,16,32]{0,1,2:T(8,128)(2,1)S(1)} %copy.36), channel_id=1, replica_groups=mesh['site'=2,'row'=4,'col'=4] {'col'}, dimensions={1}, use_global_device_ids=true | all-gather | bytes 327680 | tf_op jit(solution)/shard_map/all_gather | solution.py:44
  33.4 0.4 fusion.1
  33.8 0.3 copy.38
  34.1 0.3 reshape.43
  34.4 8.1 %all_to_all.45 = bf16[4,2,4096]{2,1,0:T(2,128)(2,1)S(1)} all-to-all(bf16[4,2,4096]{2,1,0:T(2,128)(2,1)S(1)} %reshape.43), channel_id=1, replica_groups=mesh['site'=2,'row'=4,'col'=4] {'row'}, dimensions={0} | all-to-all | bytes 131072 | tf_op jit(solution)/shard_map/all_to_all | solution.py:49
  42.5 0.2 reshape.44
  42.7 0.1 fusion.7
  42.8 0.2 multiply_reduce_fusion
  43.1 0.3 copy.39
  43.4 0.0 copy-start.5
  43.5 0.3 reshape.32
  43.7 0.4 copy-done.5
  44.1 0.0 copy-start.3
  44.1 0.1 multiply_convert_fusion
  44.2 0.6 %copy-done.3 = bf16[128,128]{1,0:T(8,128)(2,1)S(1)} copy-done((bf16[128,128]{1,0:T(8,128)(2,1)S(1)}, bf16[128,128]{1,0:T(8,128)(2,1)}, u32[]{:S(2)}) %copy-start.3) | copy-done | bytes 32792
  44.9 0.0 copy-start.6
  44.9 0.1 fusion.14
  45.0 0.6 %copy-done.6 = bf16[128,128]{1,0:T(8,128)(2,1)S(1)} copy-done((bf16[128,128]{1,0:T(8,128)(2,1)S(1)}, bf16[128,128]{1,0:T(8,128)(2,1)}, u32[]{:S(2)}) %copy-start.6) | copy-done | bytes 32792
  45.6 0.8 %fusion.6 = bf16[16,16,128]{2,1,0:T(8,128)(2,1)} fusion(f32[16,16,128]{2,1,0:T(8,128)S(1)} %fusion.14, bf16[16,16,128]{2,1,0:T(8,128)(2,1)S(1)} %fusion.12, bf16[128,128]{1,0:T(8,128)(2,1)S(1)} %copy-done.6), kind=kOutput, calls=%fused_computation.8 | convolution fusion | flops 8552448 | bytes 294912 | tf_op jit(solution)/shard_map/ijc,cd->ijd/dot_general | solution.py:28
  (5 shorter events, 0.1 us)
Async XLA Ops:
  0.0 2.0 %copy-start = (bf16[128,128]{1,0:T(8,128)(2,1)S(1)}, bf16[128,128]{1,0:T(8,128)(2,1)}, u32[]{:S(2)}) copy-start(bf16[128,128]{1,0:T(8,128)(2,1)} %param.10) | copy-start | bytes 98308
  0.0 1.0 %copy-start.1 = (bf16[16,16,128]{2,1,0:T(8,128)(2,1)S(1)}, bf16[16,16,128]{2,1,0:T(8,128)(2,1)}, u32[]{:S(2)}) copy-start(bf16[16,16,128]{2,1,0:T(8,128)(2,1)} %param.7) | copy-start | bytes 196612
  1.2 0.7 %copy-start.4 = (f32[128]{0:T(128)S(1)}, f32[128]{0:T(128)}, u32[]{:S(2)}) copy-start(f32[128]{0:T(128)} %param.8) | copy-start | bytes 1540
  3.8 6.5 %copy-start.2 = (bf16[128,128]{1,0:T(8,128)(2,1)S(1)}, bf16[128,128]{1,0:T(8,128)(2,1)}, u32[]{:S(2)}) copy-start(bf16[128,128]{1,0:T(8,128)(2,1)} %param.9) | copy-start | bytes 98308
  3.8 12.2 %all-to-all-start = ((bf16[4,2,4096]{2,1,0:T(2,128)(2,1)}), bf16[4,2,4096]{2,1,0:T(2,128)(2,1)S(1)}, u32[]{:S(2)}, u32[]{:S(2)}) async-start(bf16[4,2,4096]{2,1,0:T(2,128)(2,1)} %reshape.39), calls=%async_computation | async-start | bytes 131072 | tf_op jit(solution)/shard_map/all_to_all | solution.py:40
  16.0 9.0 %all-to-all-start.1 = ((bf16[4,2,4096]{2,1,0:T(2,128)(2,1)}), bf16[4,2,4096]{2,1,0:T(2,128)(2,1)S(1)}, u32[]{:S(2)}, u32[]{:S(2)}) async-start(bf16[4,2,4096]{2,1,0:T(2,128)(2,1)} %reshape.41), calls=%async_computation.1 | async-start | bytes 131072 | tf_op jit(solution)/shard_map/all_to_all | solution.py:39
  43.4 0.7 %copy-start.5 = (f32[128]{0:T(128)S(1)}, f32[128]{0:T(128)}, u32[]{:S(2)}) copy-start(f32[128]{0:T(128)} %param.11) | copy-start | bytes 1540
  44.1 0.8 %copy-start.3 = (bf16[128,128]{1,0:T(8,128)(2,1)S(1)}, bf16[128,128]{1,0:T(8,128)(2,1)}, u32[]{:S(2)}) copy-start(bf16[128,128]{1,0:T(8,128)(2,1)} %param.12) | copy-start | bytes 98308
  44.9 0.8 %copy-start.6 = (bf16[128,128]{1,0:T(8,128)(2,1)S(1)}, bf16[128,128]{1,0:T(8,128)(2,1)}, u32[]{:S(2)}) copy-start(bf16[128,128]{1,0:T(8,128)(2,1)} %param.13) | copy-start | bytes 98308
where the time goes:
time: 47 us; the launch traced here: 46.4 us
  blocking collectives  15.3 us (33%)
  starting transfers between devices  9.76 us (21%)
  local copies, waits for them, and re-layouts  9.11 us (19%)
  waiting for transfers between devices  8.55 us (18%)
  other arithmetic  1.87 us (4%)
  matrix products  1.61 us (3%)
    all_to_all x1, blocking collectives, body(): lax.all_to_all(strip, 'row', split_axis=0, concat_axis=2, tiled=True)  8.11 us
    all_gather x1, blocking collectives, body(): lax.all_gather(left_lines, 'col', axis=1, tiled=True)  7.2 us
    all_to_all x1, starting transfers between devices, body(): lax.all_to_all(right, 'row', split_axis=2, concat_axis=0, tiled=True)  6.48 us
    unnamed x20, local copies, waits for them, and re-layouts  5.82 us
    all_to_all x1, waiting for transfers between devices, body(): lax.all_to_all(left, 'row', split_axis=2, concat_axis=0, tiled=True)  4.56 us
    all_to_all x1, waiting for transfers between devices, body(): lax.all_to_all(right, 'row', split_axis=2, concat_axis=0, tiled=True)  3.99 us
    all_to_all x1, starting transfers between devices, body(): lax.all_to_all(left, 'row', split_axis=2, concat_axis=0, tiled=True)  3.28 us
    reduce_sum x2, other arithmetic, norm_channels(): centred = values - jnp.mean(values, axis=-1, keepdims=True)  1.14 us
  transfers between devices with their start and end apart: 2, of which 2 were waited for; matrix products, arithmetic and copies ran while one was open for 6% of the time, Pallas kernels for 0%

commit v1 on v0

--- a/solution.py
+++ b/solution.py
@@ -41,7 +41,9 @@
     )
     strip = jnp.einsum(
         "kid,kjd->ijd",
-        lax.all_gather(left_lines, "col", axis=1, tiled=True),
+        jnp.concatenate(
+            lax.all_to_all(jnp.stack([left_lines] * lax.axis_size("col")), "col", 0, 0), axis=1
+        ),
         right_lines,
         preferred_element_type=jnp.float32,
     )

time: 47 us -> 48.5 us (1.032)
  blocking collectives: 15.3 us -> 8.11 us
  waiting for transfers between devices: 8.55 us -> 12.2 us
  starting transfers between devices: 9.76 us -> 13.2 us
  local copies, waits for them, and re-layouts: 9.11 us -> 10.6 us
    all_gather x1 -> x0, blocking collectives: 7.2 us -> none  [body(): lax.all_gather(left_lines, 'col', axis=1, tiled=True)]
    all_to_all x0 -> x1, waiting for transfers between devices: none -> 4.82 us  [body(): lax.all_to_all(jnp.stack([left_lines] * lax.axis_size('col')), 'col', 0, 0)]
    all_to_all x0 -> x1, starting transfers between devices: none -> 3.4 us  [body(): lax.all_to_all(jnp.stack([left_lines] * lax.axis_size('col')), 'col', 0, 0)]
    all_to_all x1, starting transfers between devices: 3.28 us -> 6.48 us  [body(): lax.all_to_all(left, 'row', split_axis=2, concat_axis=0, tiled=True)]
    all_to_all x1, starting transfers between devices: 6.48 us -> 3.29 us  [body(): lax.all_to_all(right, 'row', split_axis=2, concat_axis=0, tiled=True)]
    unnamed x20 -> x23, local copies, waits for them, and re-layouts: 5.82 us -> 7.32 us
    all_to_all x1, waiting for transfers between devices: 4.56 us -> 3.99 us  [body(): lax.all_to_all(left, 'row', split_axis=2, concat_axis=0, tiled=True)]
    all_to_all x1, waiting for transfers between devices: 3.99 us -> 3.44 us  [body(): lax.all_to_all(right, 'row', split_axis=2, concat_axis=0, tiled=True)]
  transfers between devices with their start and end apart: 2 -> 3, of which waited for: 2 -> 3; matrix products, arithmetic and copies ran while one was open for 6% -> 11% of each run, Pallas kernels for 0% -> 0%
where the time goes in v1:
time: 48.5 us; the launch traced here: 47.8 us
  starting transfers between devices  13.2 us (27%)
  waiting for transfers between devices  12.2 us (25%)
  local copies, waits for them, and re-layouts  10.6 us (22%)
  blocking collectives  8.11 us (17%)
  other arithmetic  1.87 us (4%)
  matrix products  1.61 us (3%)
    all_to_all x1, blocking collectives, body(): lax.all_to_all(strip, 'row', split_axis=0, concat_axis=2, tiled=True)  8.11 us
    unnamed x23, local copies, waits for them, and re-layouts  7.32 us
    all_to_all x1, starting transfers between devices, body(): lax.all_to_all(left, 'row', split_axis=2, concat_axis=0, tiled=True)  6.48 us
    all_to_all x1, waiting for transfers between devices, body(): lax.all_to_all(jnp.stack([left_lines] * lax.axis_size('col')), 'col', 0, 0)  4.82 us
    all_to_all x1, waiting for transfers between devices, body(): lax.all_to_all(left, 'row', split_axis=2, concat_axis=0, tiled=True)  3.99 us
    all_to_all x1, waiting for transfers between devices, body(): lax.all_to_all(right, 'row', split_axis=2, concat_axis=0, tiled=True)  3.44 us
    all_to_all x1, starting transfers between devices, body(): lax.all_to_all(jnp.stack([left_lines] * lax.axis_size('col')), 'col', 0, 0)  3.4 us
    all_to_all x1, starting transfers between devices, body(): lax.all_to_all(right, 'row', split_axis=2, concat_axis=0, tiled=True)  3.29 us
  transfers between devices with their start and end apart: 3, of which 3 were waited for; matrix products, arithmetic and copies ran while one was open for 11% of the time, Pallas kernels for 0%

profile of v1, /device:TPU:0, one launch (start us, length us, event | category | flops | bytes accessed | tf_op | source)
XLA Modules:
  0.0 47.8 jit_solution(10338723388784889439)
XLA Ops:
  0.0 0.0 copy-start
  0.0 0.0 copy-start.1
  0.0 1.0 %convert_reduce_fusion = f32[16,16]{1,0:T(8,128)S(1)} fusion(bf16[16,16,128]{2,1,0:T(8,128)(2,1)} %param.7), kind=kLoop, calls=%fused_computation.16 | loop fusion | flops 65280 | bytes 66560 | tf_op jit(solution)/shard_map/reduce_sum | solution.py:8
  1.0 0.0 copy-done.1
  1.0 0.2 fusion.11
  1.2 0.0 copy-start.4
  1.3 0.6 %copy-done.4 = f32[128]{0:T(128)S(1)} copy-done((f32[128]{0:T(128)S(1)}, f32[128]{0:T(128)}, u32[]{:S(2)}) %copy-start.4) | copy-done | bytes 536
  1.9 0.1 fusion.13
  2.0 0.0 copy-done
  2.0 0.1 convolution_convert_fusion
  2.2 0.4 copy.36
  2.6 1.2 %reshape.52 = bf16[4,2,4096]{2,1,0:T(2,128)(2,1)} reshape(bf16[128,16,16]{2,1,0:T(8,128)(2,1)S(1)} %bitcast.49) | data formatting | bytes 131072
  3.8 0.0 copy-start.2
  3.8 6.5 %all-to-all-start.1 = ((bf16[4,2,4096]{2,1,0:T(2,128)(2,1)}), bf16[4,2,4096]{2,1,0:T(2,128)(2,1)S(1)}, u32[]{:S(2)}, u32[]{:S(2)}) async-start(bf16[4,2,4096]{2,1,0:T(2,128)(2,1)} %reshape.52), calls=%async_computation.1 | async-start | bytes 131072 | tf_op jit(solution)/shard_map/all_to_all | solution.py:39
  10.3 0.0 copy-done.2
  10.3 0.1 convolution_convert_fusion.1
  10.4 0.4 copy.34
  10.9 1.2 %reshape.50 = bf16[4,2,4096]{2,1,0:T(2,128)(2,1)} reshape(bf16[128,16,16]{2,1,0:T(8,128)(2,1)S(1)} %bitcast.50) | data formatting | bytes 131072
  12.0 4.0 %all-to-all-done.1 = bf16[4,2,4096]{2,1,0:T(2,128)(2,1)S(1)} async-done(((bf16[4,2,4096]{2,1,0:T(2,128)(2,1)}), bf16[4,2,4096]{2,1,0:T(2,128)(2,1)S(1)}, u32[]{:S(2)}, u32[]{:S(2)}) %all-to-all-start.1) | async-done | bytes 65568 | tf_op jit(solution)/shard_map/all_to_all | solution.py:39
  16.0 3.3 %all-to-all-start = ((bf16[4,2,4096]{2,1,0:T(2,128)(2,1)}), bf16[4,2,4096]{2,1,0:T(2,128)(2,1)S(1)}, u32[]{:S(2)}, u32[]{:S(2)}) async-start(bf16[4,2,4096]{2,1,0:T(2,128)(2,1)} %reshape.50), calls=%async_computation | async-start | bytes 131072 | tf_op jit(solution)/shard_map/all_to_all | solution.py:40
  19.3 0.4 reshape.53
  19.7 0.4 copy.37
  20.1 0.3 copy.38
  20.4 0.1 broadcast_bitcast_fusion
  20.5 1.1 %reshape.54 = bf16[4,2,16384]{2,1,0:T(2,128)(2,1)} reshape(bf16[4,16,32,64]{3,2,1,0:T(8,128)(2,1)S(1)} %broadcast_bitcast_fusion) | data formatting | bytes 524288
  21.6 3.4 %all-to-all-done = bf16[4,2,4096]{2,1,0:T(2,128)(2,1)S(1)} async-done(((bf16[4,2,4096]{2,1,0:T(2,128)(2,1)}), bf16[4,2,4096]{2,1,0:T(2,128)(2,1)S(1)}, u32[]{:S(2)}, u32[]{:S(2)}) %all-to-all-start) | async-done | bytes 65568 | tf_op jit(solution)/shard_map/all_to_all | solution.py:40
  25.0 3.4 %all-to-all-start.2 = ((bf16[4,2,16384]{2,1,0:T(2,128)(2,1)}), bf16[4,2,16384]{2,1,0:T(2,128)(2,1)S(1)}, u32[]{:S(2)}, u32[]{:S(2)}) async-start(bf16[4,2,16384]{2,1,0:T(2,128)(2,1)} %reshape.54), calls=%async_computation.2 | async-start | bytes 524288 | tf_op jit(solution)/shard_map/all_to_all | solution.py:45
  28.4 0.4 reshape.51
  28.8 0.4 copy.35
  29.3 0.3 copy.39
  29.6 4.8 %all-to-all-done.2 = bf16[4,2,16384]{2,1,0:T(2,128)(2,1)S(1)} async-done(((bf16[4,2,16384]{2,1,0:T(2,128)(2,1)}), bf16[4,2,16384]{2,1,0:T(2,128)(2,1)S(1)}, u32[]{:S(2)}, u32[]{:S(2)}) %all-to-all-start.2) | async-done | bytes 262176 | tf_op jit(solution)/shard_map/all_to_all | solution.py:45
  34.4 0.3 reshape.55
  34.8 0.4 fusion.1
  35.1 0.3 copy.41
  35.4 0.3 reshape.56
  35.7 8.1 %all_to_all.47 = bf16[4,2,4096]{2,1,0:T(2,128)(2,1)S(1)} all-to-all(bf16[4,2,4096]{2,1,0:T(2,128)(2,1)S(1)} %reshape.56), channel_id=1, replica_groups=mesh['site'=2,'row'=4,'col'=4] {'row'}, dimensions={0} | all-to-all | bytes 131072 | tf_op jit(solution)/shard_map/all_to_all | solution.py:51
  43.8 0.2 reshape.57
  44.1 0.1 fusion.8
  44.2 0.2 multiply_reduce_fusion
  44.5 0.3 copy.42
  44.8 0.0 copy-start.5
  44.8 0.3 reshape.43
  45.1 0.4 copy-done.5
  45.5 0.1 multiply_convert_fusion
  45.6 0.6 %copy-done.3 = bf16[128,128]{1,0:T(8,128)(2,1)S(1)} copy-done((bf16[128,128]{1,0:T(8,128)(2,1)S(1)}, bf16[128,128]{1,0:T(8,128)(2,1)}, u32[]{:S(2)}) %copy-start.3) | copy-done | bytes 32792
  46.2 0.1 fusion.15
  46.4 0.6 %copy-done.6 = bf16[128,128]{1,0:T(8,128)(2,1)S(1)} copy-done((bf16[128,128]{1,0:T(8,128)(2,1)S(1)}, bf16[128,128]{1,0:T(8,128)(2,1)}, u32[]{:S(2)}) %copy-start.6) | copy-done | bytes 32792
  47.0 0.8 %fusion.6 = bf16[16,16,128]{2,1,0:T(8,128)(2,1)} fusion(f32[16,16,128]{2,1,0:T(8,128)S(1)} %fusion.15, bf16[16,16,128]{2,1,0:T(8,128)(2,1)S(1)} %fusion.13, bf16[128,128]{1,0:T(8,128)(2,1)S(1)} %copy-done.6), kind=kOutput, calls=%fused_computation.8 | convolution fusion | flops 8552448 | bytes 294912 | tf_op jit(solution)/shard_map/ijc,cd->ijd/dot_general | solution.py:28
  (7 shorter events, 0.1 us)
Async XLA Ops:
  0.0 2.0 %copy-start = (bf16[128,128]{1,0:T(8,128)(2,1)S(1)}, bf16[128,128]{1,0:T(8,128)(2,1)}, u32[]{:S(2)}) copy-start(bf16[128,128]{1,0:T(8,128)(2,1)} %param.9) | copy-start | bytes 98308
  0.0 1.0 %copy-start.1 = (bf16[16,16,128]{2,1,0:T(8,128)(2,1)S(1)}, bf16[16,16,128]{2,1,0:T(8,128)(2,1)}, u32[]{:S(2)}) copy-start(bf16[16,16,128]{2,1,0:T(8,128)(2,1)} %param.7) | copy-start | bytes 196612
  1.2 0.7 %copy-start.4 = (f32[128]{0:T(128)S(1)}, f32[128]{0:T(128)}, u32[]{:S(2)}) copy-start(f32[128]{0:T(128)} %param.8) | copy-start | bytes 1540
  3.8 6.5 %copy-start.2 = (bf16[128,128]{1,0:T(8,128)(2,1)S(1)}, bf16[128,128]{1,0:T(8,128)(2,1)}, u32[]{:S(2)}) copy-start(bf16[128,128]{1,0:T(8,128)(2,1)} %param.10) | copy-start | bytes 98308
  3.8 12.2 %all-to-all-start.1 = ((bf16[4,2,4096]{2,1,0:T(2,128)(2,1)}), bf16[4,2,4096]{2,1,0:T(2,128)(2,1)S(1)}, u32[]{:S(2)}, u32[]{:S(2)}) async-start(bf16[4,2,4096]{2,1,0:T(2,128)(2,1)} %reshape.52), calls=%async_computation.1 | async-start | bytes 131072 | tf_op jit(solution)/shard_map/all_to_all | solution.py:39
  16.0 9.0 %all-to-all-start = ((bf16[4,2,4096]{2,1,0:T(2,128)(2,1)}), bf16[4,2,4096]{2,1,0:T(2,128)(2,1)S(1)}, u32[]{:S(2)}, u32[]{:S(2)}) async-start(bf16[4,2,4096]{2,1,0:T(2,128)(2,1)} %reshape.50), calls=%async_computation | async-start | bytes 131072 | tf_op jit(solution)/shard_map/all_to_all | solution.py:40
  25.0 9.4 %all-to-all-start.2 = ((bf16[4,2,16384]{2,1,0:T(2,128)(2,1)}), bf16[4,2,16384]{2,1,0:T(2,128)(2,1)S(1)}, u32[]{:S(2)}, u32[]{:S(2)}) async-start(bf16[4,2,16384]{2,1,0:T(2,128)(2,1)} %reshape.54), calls=%async_computation.2 | async-start | bytes 524288 | tf_op jit(solution)/shard_map/all_to_all | solution.py:45
  44.8 0.7 %copy-start.5 = (f32[128]{0:T(128)S(1)}, f32[128]{0:T(128)}, u32[]{:S(2)}) copy-start(f32[128]{0:T(128)} %param.11) | copy-start | bytes 1540
  45.5 0.8 %copy-start.3 = (bf16[128,128]{1,0:T(8,128)(2,1)S(1)}, bf16[128,128]{1,0:T(8,128)(2,1)}, u32[]{:S(2)}) copy-start(bf16[128,128]{1,0:T(8,128)(2,1)} %param.12) | copy-start | bytes 98308
  46.2 0.8 %copy-start.6 = (bf16[128,128]{1,0:T(8,128)(2,1)S(1)}, bf16[128,128]{1,0:T(8,128)(2,1)}, u32[]{:S(2)}) copy-start(bf16[128,128]{1,0:T(8,128)(2,1)} %param.13) | copy-start | bytes 98308
